TPU v7x, 128 devices: a whole 4x4x4 slice. The times are simulated.
128 devices in a mesh: model: 16 (over z, y), fsdp: 8 (over x, core).
Axes of the slice: x: 4, y: 4, z: 4, core: 2. Of those that a mesh axis runs over, the one named last changes fastest.
Arguments:
- tok_ids: int32 [8, 2048], P('fsdp')
- tok_labels: int32 [8, 2048], P('fsdp')
- emb_table: bfloat16 [32128, 768], P(('model', 'fsdp'))
- w_gate: bfloat16 [768, 2048], P('fsdp')
- w_up: bfloat16 [768, 2048], P('fsdp')
- w_down: bfloat16 [2048, 768], P('fsdp')
- gain_in: float32 [768], replicated
- gain_out: float32 [768], replicated
Outputs:
- output 1: float32 [], replicated
- output 2: float32 [32128, 768], P(('model', 'fsdp'))
- output 3: float32 [768, 2048], P('fsdp')
- output 4: float32 [768, 2048], P('fsdp')
- output 5: float32 [2048, 768], P('fsdp')
All inputs are finite; a program needn't handle non-finite values.
Results may differ from a plain program's by a relative error of at most 0.00822918.
Values are sent between devices in bfloat16 or wider.
A program may use at most 1 GiB of HBM per device.

v0:
```python
import jax
import jax.numpy as jnp
from jax import lax
from jax.sharding import PartitionSpec as P

EPS = 1e-6


def rms_scale(values, gain_vec):
    mean_sq = jnp.mean(values * values, axis=-1, keepdims=True)
    return values * lax.rsqrt(mean_sq + EPS) * gain_vec


def mlp_forward(x_emb, gain_in, w_gate, w_up, w_down):
    normed_in, norm_in_back = jax.vjp(lambda values: rms_scale(values, gain_in), x_emb)
    normed_bf = normed_in.astype(jnp.bfloat16)
    gate_f = jnp.dot(normed_bf, w_gate, preferred_element_type=jnp.float32).astype(jnp.bfloat16).astype(jnp.float32)
    up_f = jnp.dot(normed_bf, w_up, preferred_element_type=jnp.float32).astype(jnp.bfloat16).astype(jnp.float32)
    gate_sig = jax.nn.sigmoid(gate_f)
    silu_gate = gate_f * gate_sig
    act_bf = (silu_gate * up_f).astype(jnp.bfloat16)
    mlp_out = jnp.dot(act_bf, w_down, preferred_element_type=jnp.float32).astype(jnp.bfloat16)
    h_res = x_emb + mlp_out.astype(jnp.float32)
    return h_res, (norm_in_back, normed_bf, gate_f, up_f, gate_sig, silu_gate, act_bf)


def mlp_backward(d_hidden, saved, w_gate, w_up, w_down):
    norm_in_back, normed_bf, gate_f, up_f, gate_sig, silu_gate, act_bf = saved
    d_mlp = d_hidden.astype(jnp.bfloat16)
    d_act = jnp.einsum("td,fd->tf", d_mlp, w_down, preferred_element_type=jnp.float32)
    grad_down = jnp.einsum("tf,td->fd", act_bf, d_mlp, preferred_element_type=jnp.float32)
    d_gate = (d_act * up_f * (gate_sig * (1.0 + gate_f * (1.0 - gate_sig)))).astype(jnp.bfloat16)
    d_up = (d_act * silu_gate).astype(jnp.bfloat16)
    grad_gate = jnp.einsum("td,tf->df", normed_bf, d_gate, preferred_element_type=jnp.float32)
    grad_up = jnp.einsum("td,tf->df", normed_bf, d_up, preferred_element_type=jnp.float32)
    d_normed = jnp.einsum("tf,df->td", d_gate, w_gate, preferred_element_type=jnp.float32) + jnp.einsum("tf,df->td", d_up, w_up, preferred_element_type=jnp.float32)
    d_x = d_hidden + norm_in_back(d_normed)[0]
    return d_x, grad_gate, grad_up, grad_down


def solution(mesh):
    fsdp_size = mesh.shape["fsdp"]
    tok_spec = P("fsdp", None)
    row_spec = P(("model", "fsdp"), None)
    weight_spec = P("fsdp", None)

    def device_step(tok_ids, tok_labels, table_shard, gate_shard, up_shard, down_shard, gain_in, gain_out):
        local_count = tok_ids.shape[0] * tok_ids.shape[1]
        num_tokens = local_count * fsdp_size
        table_part = lax.all_gather(table_shard, "fsdp", axis=0, tiled=True)
        w_gate = lax.all_gather(gate_shard, "fsdp", axis=0, tiled=True)
        w_up = lax.all_gather(up_shard, "fsdp", axis=0, tiled=True)
        w_down = lax.all_gather(down_shard, "fsdp", axis=0, tiled=True)
        vocab_part = table_part.shape[0]
        vocab_start = lax.axis_index("model") * vocab_part
        local_ids = tok_ids.reshape(local_count) - vocab_start
        id_inside = (local_ids >= 0) & (local_ids < vocab_part)
        safe_ids = jnp.where(id_inside, local_ids, 0)
        emb_rows = jnp.where(id_inside[:, None], jnp.take(table_part, safe_ids, axis=0), 0)
        x_emb = lax.psum(emb_rows, "model").astype(jnp.float32)
        h_res, saved = mlp_forward(x_emb, gain_in, w_gate, w_up, w_down)
        hn_f, norm_out_back = jax.vjp(lambda values: rms_scale(values, gain_out), h_res)
        hn_bf = hn_f.astype(jnp.bfloat16)
        logits = jnp.einsum("td,vd->tv", hn_bf, table_part, preferred_element_type=jnp.float32)
        row_max = lax.pmax(jnp.max(logits, axis=-1), "model")
        exp_shift = jnp.exp(logits - row_max[:, None])
        local_labels = tok_labels.reshape(local_count) - vocab_start
        onehot = lax.broadcasted_iota(jnp.int32, logits.shape, 1) == local_labels[:, None]
        part_stats = jnp.stack([jnp.sum(exp_shift, axis=-1), jnp.sum(jnp.where(onehot, logits, 0.0), axis=-1)])
        tok_stats = lax.psum(part_stats, "model")
        sum_exp = tok_stats[0]
        tok_loss = row_max + jnp.log(sum_exp) - tok_stats[1]
        loss = lax.psum(jnp.sum(tok_loss), "fsdp") / num_tokens
        soft_probs = exp_shift / sum_exp[:, None]
        d_logits = (jnp.where(onehot, soft_probs - 1.0, soft_probs) / num_tokens).astype(jnp.bfloat16)
        d_head = jnp.einsum("tv,td->vd", d_logits, hn_bf, preferred_element_type=jnp.float32)
        d_hn = lax.psum(jnp.einsum("tv,vd->td", d_logits, table_part, preferred_element_type=jnp.float32), "model")
        d_hidden = norm_out_back(d_hn)[0]
        d_x, grad_gate, grad_up, grad_down = mlp_backward(d_hidden, saved, w_gate, w_up, w_down)
        d_in = jax.ops.segment_sum(jnp.where(id_inside[:, None], d_x, 0.0), safe_ids, num_segments=vocab_part)
        grad_table = lax.psum_scatter(d_head + d_in, "fsdp", scatter_dimension=0, tiled=True)
        grad_gate = lax.psum_scatter(grad_gate, "fsdp", scatter_dimension=0, tiled=True)
        grad_up = lax.psum_scatter(grad_up, "fsdp", scatter_dimension=0, tiled=True)
        grad_down = lax.psum_scatter(grad_down, "fsdp", scatter_dimension=0, tiled=True)
        return loss, grad_table, grad_gate, grad_up, grad_down

    return jax.shard_map(device_step, mesh=mesh, in_specs=(tok_spec, tok_spec, row_spec, weight_spec, weight_spec, weight_spec, P(), P()), out_specs=(P(), row_spec, weight_spec, weight_spec, weight_spec), check_vma=False)
```

profile of v0, /device:TPU:1, one launch (start us, length us, event | category | flops | bytes accessed | tf_op | source)
XLA Modules:
  0.0 752.2 jit_solution(6535928463872732308)
XLA Ops:
  9.3 31.4 %all-gather.12.cloned.1.call-done = bf16[8,251,768]{2,1,0:T(8,128)(2,1)} async-done(((bf16[1,251,768]{2,1,0:T(8,128)(2,1)}), bf16[8,251,768]{2,1,0:T(8,128)(2,1)}) %all-gather.12.cloned.1.call-update) | async-done | bytes 3084304 | tf_op jit(solution)/shard_map/all_gather | solution.py:50
  43.5 9.4 %gather_fusion = bf16[2048,768]{1,0:T(8,128)(2,1)} fusion(bf16[2008,768]{1,0:T(8,128)(2,1)S(1)} %reshape.120, s32[2048]{0:T(1024)S(1)} %broadcast_clamp_fusion), kind=kCustom, calls=%fused_computation | custom fusion | bytes 6299648 | tf_op jit(solution)/shard_map/jit(_take)/gather | solution.py:59
  63.9 92.7 %all-reduce.5.cloned.1.call-done = bf16[2048,768]{0,1:T(8,128)(2,1)} async-done(((bf16[2048,768]{0,1:T(8,128)(2,1)}), bf16[2048,768]{0,1:T(8,128)(2,1)}) %all-reduce.5.cloned.1.call-update) | async-done | bytes 3145744 | tf_op jit(solution)/shard_map/psum | solution.py:60
  159.2 26.3 %all-gather.6.cloned.1.call-done = bf16[768,2048]{1,0:T(8,128)(2,1)} async-done(((bf16[96,2048]{1,0:T(8,128)(2,1)}), bf16[768,2048]{1,0:T(8,128)(2,1)}) %all-gather.6.cloned.1.call-update) | async-done | bytes 3145744 | tf_op jit(solution)/shard_map/all_gather | solution.py:51
  185.5 11.7 %convolution_convert_fusion.1 = bf16[2048,2048]{1,0:T(8,128)(2,1)} fusion(bf16[768,2048]{1,0:T(8,128)(2,1)} %all-gather.6.cloned.1.call-done, bf16[2048,768]{0,1:T(8,128)(2,1)} %all-reduce.5.cloned.1.call-done, f32[768]{0:T(1024)S(1)} %copy-done.23, f32[2048]{0:T(1024)S(1)} %fusion.22), kind=kOutput, calls=%fused_computation.31 | convolution fusion | flops 6452936704 | bytes 14691328 | tf_op jit(solution)/shard_map/dot_general | solution.py:17
  197.2 17.5 %all-gather.8.cloned.1.call-done = bf16[768,2048]{1,0:T(8,128)(2,1)} async-done(((bf16[96,2048]{1,0:T(8,128)(2,1)}), bf16[768,2048]{1,0:T(8,128)(2,1)}) %all-gather.8.cloned.1.call-update) | async-done | bytes 3145744 | tf_op jit(solution)/shard_map/all_gather | solution.py:52
  214.6 17.3 %fusion.1 = (bf16[2048,2048]{1,0:T(8,128)(2,1)}, bf16[2048,2048]{1,0:T(8,128)(2,1)}) fusion(bf16[2048,2048]{1,0:T(8,128)(2,1)} %convolution_convert_fusion.1, bf16[768,2048]{1,0:T(8,128)(2,1)} %all-gather.8.cloned.1.call-done, bf16[2048,768]{0,1:T(8,128)(2,1)} %all-reduce.5.cloned.1.call-done, f32[768]{0:T(1024)S(1)} %copy-done.23, f32[2048]{0:T(1024)S(1)} %fusion.22), kind=kOutput, calls=%fused_computation.8 | convolution fusion | flops 6486491136 | bytes 31468544 | tf_op jit(solution)/shard_map/dot_general | solution.py:18
  231.9 11.9 %all-gather.10.cloned.1.call-done = bf16[2048,768]{1,0:T(8,128)(2,1)} async-done(((bf16[256,768]{1,0:T(8,128)(2,1)}), bf16[2048,768]{1,0:T(8,128)(2,1)}) %all-gather.10.cloned.1.call-update) | async-done | bytes 3145744 | tf_op jit(solution)/shard_map/all_gather | solution.py:53
  243.8 12.3 %multiply_reduce_fusion.1 = (f32[2048]{0:T(1024)S(1)}, bf16[2048,768]{0,1:T(8,128)(2,1)S(1)}) fusion(bf16[2048,768]{0,1:T(8,128)(2,1)} %all-reduce.5.cloned.1.call-done, bf16[2048,2048]{1,0:T(8,128)(2,1)} %get-tuple-element.16, bf16[2048,768]{1,0:T(8,128)(2,1)} %all-gather.10.cloned.1.call-done), kind=kOutput, calls=%fused_computation.41 | convolution fusion | flops 6451886080 | bytes 17833984 | tf_op jit(solution)/shard_map/dot_general | solution.py:22
  256.2 10.5 %fusion.33 = (f32[2048]{0:T(1024)S(1)}, f32[2048,2008]{0,1:T(8,128)}) fusion(bf16[2008,768]{1,0:T(8,128)(2,1)S(1)} %reshape.120, bf16[2048,768]{0,1:T(8,128)(2,1)S(1)} %get-tuple-element.19, bf16[2048,768]{0,1:T(8,128)(2,1)S(1)} %copy-done, f32[768]{0:T(1024)S(1)} %copy-done.17, f32[2048]{0:T(1024)S(1)} %fusion.23), kind=kOutput, calls=%fused_computation.70 | convolution fusion | flops 6330169344 | bytes 25844736 | tf_op jit(solution)/shard_map/td,vd->tv/dot_general | solution.py:64
  266.7 33.9 %pmax.7 = f32[2048]{0:T(1024)S(1)} all-reduce(f32[2048]{0:T(1024)S(1)} %get-tuple-element.20), channel_id=1, replica_groups=mesh['model'=16,'fsdp'=8] {'model'}, use_global_device_ids=true, to_apply=%region_4.5 | all-reduce | flops 2048 | bytes 16384 | tf_op jit(solution)/shard_map/pmax | solution.py:65
  308.7 56.2 %psum.29 = f32[2,2048]{1,0:T(2,128)S(1)} all-reduce(f32[2,2048]{1,0:T(2,128)S(1)} %pad_maximum_fusion), channel_id=1, replica_groups=mesh['model'=16,'fsdp'=8] {'model'}, use_global_device_ids=true, to_apply=%region_7.8 | all-reduce | flops 4096 | bytes 32768 | tf_op jit(solution)/shard_map/psum | solution.py:70
  377.7 9.1 %fusion.34 = f32[2048,768]{0,1:T(8,128)} fusion(bf16[2048,2008]{0,1:T(8,128)(2,1)S(1)} %fusion.10, bf16[2008,768]{1,0:T(8,128)(2,1)S(1)} %reshape.120), kind=kOutput, calls=%fused_computation.71 | convolution fusion | flops 6316621824 | bytes 17600512 | tf_op jit(solution)/shard_map/tv,vd->td/dot_general | solution.py:77
  386.9 137.7 %all-reduce.7.cloned.1.call-done = f32[2048,768]{0,1:T(8,128)} async-done(((f32[2048,768]{0,1:T(8,128)}), f32[2048,768]{0,1:T(8,128)}) %all-reduce.7.cloned.1.call-update) | async-done | bytes 6291472 | tf_op jit(solution)/shard_map/psum | solution.py:77
  531.9 18.7 %multiply_convert_fusion = (bf16[2048,2048]{1,0:T(8,128)(2,1)}, bf16[2048,2048]{1,0:T(8,128)(2,1)}) fusion(bf16[2048,2048]{1,0:T(8,128)(2,1)} %convolution_convert_fusion.1, bf16[2048,2048]{1,0:T(8,128)(2,1)} %get-tuple-element.17, bf16[2048,768]{1,0:T(8,128)(2,1)S(1)} %copy-done.22, f32[2048]{0:T(1024)S(1)} %multiply_multiply_fusion.1, ...), kind=kOutput, calls=%fused_computation.16 | convolution fusion | flops 6519521280 | bytes 49302528 | tf_op jit(solution)/shard_map/td,fd->tf/dot_general | solution.py:30
  550.7 10.9 %fusion.28 = f32[768,2048]{1,0:T(8,128)} fusion(bf16[2048,2048]{1,0:T(8,128)(2,1)} %get-tuple-element.11, bf16[2048,768]{0,1:T(8,128)(2,1)S(1)} %copy-done.1, f32[768]{0:T(1024)S(1)} %copy-done.23, f32[2048]{0:T(1024)S(1)} %fusion.22), kind=kOutput, calls=%fused_computation.68 | convolution fusion | flops 6448742400 | bytes 17837056 | tf_op jit(solution)/shard_map/td,tf->df/dot_general | solution.py:34
  561.6 10.9 %fusion.26 = f32[768,2048]{1,0:T(8,128)} fusion(bf16[2048,2048]{1,0:T(8,128)(2,1)} %get-tuple-element.10, bf16[2048,768]{0,1:T(8,128)(2,1)S(1)} %copy-done.1, f32[768]{0:T(1024)S(1)} %copy-done.23, f32[2048]{0:T(1024)S(1)} %fusion.22), kind=kOutput, calls=%fused_computation.67 | convolution fusion | flops 6448742400 | bytes 17837056 | tf_op jit(solution)/shard_map/td,tf->df/dot_general | solution.py:35
  574.4 14.3 %fusion.18 = f32[2048,768]{1,0:T(8,128)} fusion(bf16[2048,2048]{1,0:T(8,128)(2,1)} %get-tuple-element.16, f32[2048,768]{0,1:T(8,128)} %all-reduce.7.cloned.1.call-done, bf16[2048,768]{0,1:T(8,128)(2,1)} %copy-done.3, bf16[2048,768]{0,1:T(8,128)(2,1)S(1)} %copy-done.1, f32[2048]{0:T(1024)S(1)} %multiply_multiply_fusion.1, f32[768]{0:T(1024)S(1)} %copy-done.17, ...), kind=kOutput, calls=%fused_computation.44 | convolution fusion | flops 6456606720 | bytes 27282432 | tf_op jit(solution)/shard_map/tf,td->fd/dot_general | solution.py:31
  588.7 11.9 %fusion.24 = f32[2008,768]{1,0:T(8,128)} fusion(bf16[2048,2008]{0,1:T(8,128)(2,1)} %copy-done.6, bf16[2048,768]{0,1:T(8,128)(2,1)} %copy-done.3, bf16[2048,768]{0,1:T(8,128)(2,1)S(1)} %copy-done.1, f32[768]{0:T(1024)S(1)} %copy-done.17, f32[2048]{0:T(1024)S(1)} %fusion.23), kind=kOutput, calls=%fused_computation.65 | convolution fusion | flops 6326059008 | bytes 20696064 | tf_op jit(solution)/shard_map/tv,td->vd/dot_general | solution.py:76
  600.7 11.0 %fusion.35 = f32[2048,768]{0,1:T(8,128)} fusion(bf16[2048,2048]{1,0:T(8,128)(2,1)} %get-tuple-element.11, bf16[768,2048]{1,0:T(8,128)(2,1)S(1)} %copy-done.20), kind=kOutput, calls=%fused_computation.72 | convolution fusion | flops 6442450944 | bytes 17825792 | tf_op jit(solution)/shard_map/tf,df->td/dot_general | solution.py:36
  611.7 10.7 %fusion.17 = (f32[2048]{0:T(1024)S(1)}, f32[2048,768]{0,1:T(8,128)S(1)}) fusion(bf16[2048,768]{0,1:T(8,128)(2,1)S(1)} %copy-done.1, f32[768]{0:T(1024)S(1)} %copy-done.23, f32[2048,768]{0,1:T(8,128)} %fusion.35, bf16[2048,2048]{1,0:T(8,128)(2,1)} %get-tuple-element.10, bf16[768,2048]{1,0:T(8,128)(2,1)S(1)} %copy-done.21), kind=kOutput, calls=%fused_computation.37 | convolution fusion | flops 6450313216 | bytes 27274240 | tf_op jit(solution)/shard_map/tf,df->td/dot_general | solution.py:36
  634.1 20.3 %scatter_fusion = f32[2008,768]{1,0:T(8,128)} fusion(f32[2008,768]{1,0:T(8,128)} %fusion.24, s32[2048]{0:T(1024)S(1)} %bitcast.43, f32[2048,768]{1,0:T(8,128)} %copy.20), kind=kCustom, calls=%fused_computation.1 | custom fusion | flops 1572864 | bytes 18882560 | tf_op jit(solution)/shard_map/scatter-add | solution.py:80
  654.4 69.2 %fusion = f32[256,768]{1,0:T(8,128)S(1)} fusion(f32[2008,768]{1,0:T(8,128)} %scatter_fusion), kind=kCustom, calls=%all-reduce-scatter | all-reduce-scatter fusion | flops 1572865 | bytes 6955520
  728.7 13.0 %psum.30 = f32[]{:T(128)} all-reduce(f32[]{:T(128)} %subtract_reduce_fusion), channel_id=1, replica_groups=mesh['model'=16,'fsdp'=8] {'fsdp'}, use_global_device_ids=true, to_apply=%region_9.10 | all-reduce | flops 1 | bytes 8 | tf_op jit(solution)/shard_map/psum | solution.py:73
  (100 shorter events, 66.4 us)
Async XLA Ops:
  7.2 33.6 %all-gather.12.cloned.1.call-start = ((), (), s32[]{:S(2)}) async-start(), calls=%async_computation.11 | async-start | bytes 3538944 | tf_op jit(solution)/shard_map/all_gather | solution.py:50
  7.9 148.7 %all-reduce.5.cloned.1.call-start = ((), (), s32[]{:S(2)}) async-start(), calls=%async_computation.3 | async-start | bytes 6291456 | tf_op jit(solution)/shard_map/psum | solution.py:60
  9.3 48.4 %copy-start.15 = (pred[2048]{0:T(1024)(128)(4,1)}, pred[2048]{0:T(1024)(128)(4,1)S(1)}, u32[]{:S(2)}) copy-start(pred[2048]{0:T(1024)(128)(4,1)S(1)} %get-tuple-element.14) | copy-start | bytes 6148
  57.7 127.8 %copy-start.23 = (f32[768]{0:T(1024)S(1)}, f32[768]{0:T(1024)}, u32[]{:S(2)}) copy-start(f32[768]{0:T(1024)} %param.14) | copy-start | bytes 9220
  61.7 123.8 %all-gather.6.cloned.1.call-start = ((), (), s32[]{:S(2)}) async-start(), calls=%async_computation.4 | async-start | bytes 3538944 | tf_op jit(solution)/shard_map/all_gather | solution.py:51
  62.4 152.2 %all-gather.8.cloned.1.call-start = ((), (), s32[]{:S(2)}) async-start(), calls=%async_computation.5 | async-start | bytes 3538944 | tf_op jit(solution)/shard_map/all_gather | solution.py:52
  63.0 180.8 %all-gather.10.cloned.1.call-start = ((), (), s32[]{:S(2)}) async-start(), calls=%async_computation.6 | async-start | bytes 3538944 | tf_op jit(solution)/shard_map/all_gather | solution.py:53
  63.6 461.0 %all-reduce.7.cloned.1.call-start = ((), (), s32[]{:S(2)}) async-start(), calls=%async_computation.7 | async-start | bytes 12582912 | tf_op jit(solution)/shard_map/psum | solution.py:77
  159.2 38.0 %copy-start.11 = (f32[2048]{0:T(1024)}, f32[2048]{0:T(1024)S(1)}, u32[]{:S(2)}) copy-start(f32[2048]{0:T(1024)S(1)} %fusion.14) | copy-start | bytes 24580
  243.8 12.4 %copy-start = (bf16[2048,768]{0,1:T(8,128)(2,1)S(1)}, bf16[2048,768]{0,1:T(8,128)(2,1)}, u32[]{:S(2)}) copy-start(bf16[2048,768]{0,1:T(8,128)(2,1)} %all-reduce.5.cloned.1.call-done) | copy-start | bytes 9437188
  243.8 12.4 %copy-start.17 = (f32[768]{0:T(1024)S(1)}, f32[768]{0:T(1024)}, u32[]{:S(2)}) copy-start(f32[768]{0:T(1024)} %param.15) | copy-start | bytes 9220
  300.6 64.9 %copy-start.7 = (f32[2048]{0:T(1024)}, f32[2048]{0:T(1024)S(1)}, u32[]{:S(2)}) copy-start(f32[2048]{0:T(1024)S(1)} %pmax.7) | copy-start | bytes 24580
  386.8 137.8 %copy-start.1 = (bf16[2048,768]{0,1:T(8,128)(2,1)S(1)}, bf16[2048,768]{0,1:T(8,128)(2,1)}, u32[]{:S(2)}) copy-start(bf16[2048,768]{0,1:T(8,128)(2,1)} %all-reduce.5.cloned.1.call-done) | copy-start | bytes 9437188
  386.8 357.4 %reduce-scatter.6.cloned.1.call-start = ((), (), s32[]{:S(2)}) async-start(), calls=%async_computation.8 | async-start | bytes 7077888 | tf_op jit(solution)/shard_map/reduce_scatter | solution.py:82
  561.5 182.7 %reduce-scatter.8.cloned.1.call-start = ((), (), s32[]{:S(2)}) async-start(), calls=%async_computation.9 | async-start | bytes 7077888 | tf_op jit(solution)/shard_map/reduce_scatter | solution.py:83
  572.5 171.8 %reduce-scatter.10.cloned.1.call-start = ((), (), s32[]{:S(2)}) async-start(), calls=%async_computation.10 | async-start | bytes 7077888 | tf_op jit(solution)/shard_map/reduce_scatter | solution.py:84
  588.7 11.9 %copy-start.20 = (bf16[768,2048]{1,0:T(8,128)(2,1)S(1)}, bf16[768,2048]{1,0:T(8,128)(2,1)}, u32[]{:S(2)}) copy-start(bf16[768,2048]{1,0:T(8,128)(2,1)} %all-gather.6.cloned.1.call-done) | copy-start | bytes 9437188
  600.7 11.0 %copy-start.21 = (bf16[768,2048]{1,0:T(8,128)(2,1)S(1)}, bf16[768,2048]{1,0:T(8,128)(2,1)}, u32[]{:S(2)}) copy-start(bf16[768,2048]{1,0:T(8,128)(2,1)} %all-gather.8.cloned.1.call-done) | copy-start | bytes 9437188
  600.7 21.8 %slice-start = ((s8[6291456]{0:T(1024)(128)(4,1)}), s8[4194304]{0:T(1024)(128)(4,1)S(1)}, s32[]{:S(2)}) async-start(s8[6291456]{0:T(1024)(128)(4,1)} %bitcast.31), calls=%async_computation.12 | async-start | bytes 8388608
  611.7 10.8 %copy-start.5 = (bf16[2048,768]{0,1:T(8,128)(2,1)S(1)}, bf16[2048,768]{0,1:T(8,128)(2,1)}, u32[]{:S(2)}) copy-start(bf16[2048,768]{0,1:T(8,128)(2,1)} %copy-done.3) | copy-start | bytes 9437188
  654.4 73.7 %copy-start.8 = (f32[2048]{0:T(1024)S(1)}, f32[2048]{0:T(1024)}, u32[]{:S(2)}) copy-start(f32[2048]{0:T(1024)} %copy-done.7) | copy-start | bytes 24580
  654.4 73.7 %copy-start.10 = (f32[1,2048]{1,0:T(1,128)S(1)}, f32[1,2048]{1,0:T(1,128)}, u32[]{:S(2)}) copy-start(f32[1,2048]{1,0:T(1,128)} %copy-done.9) | copy-start | bytes 24580
  654.4 73.7 %copy-start.13 = (f32[1,2048]{1,0:T(1,128)S(1)}, f32[1,2048]{1,0:T(1,128)}, u32[]{:S(2)}) copy-start(f32[1,2048]{1,0:T(1,128)} %get-tuple-element.13) | copy-start | bytes 24580
  723.7 18.7 %collective-permute-start = (f32[35,768]{1,0:T(8,128)S(1)}, f32[35,768]{1,0:T(8,128)S(1)}, u32[]{:S(2)}, u32[]{:S(2)}) collective-permute-start(f32[35,768]{1,0:T(8,128)S(1)} %slice.12), channel_id=1, source_target_pairs={{0,1},{1,2},{2,3},{3,4},{4,5},{5,6},{6,7},{8,9},{9,10},{10,11},{11... | collective-permute-start | bytes 322568
  (12 other events, 79.6 us)
Sparse Core Ops, SparseCore 0:
  9.7 31.0 all-gather.11
  61.8 94.7 all-reduce.4
  158.3 27.1 all-gather.5
  187.0 27.5 all-gather.7
  216.2 27.5 all-gather.9
  387.0 137.6 all-reduce.6
  561.7 41.9 reduce-scatter.5
  606.7 42.2 reduce-scatter.7
  651.9 69.0 reduce-scatter.9
where the time goes:
time: 755 us; the launch traced here: 752 us
  waiting for transfers between devices  320 us (42%)
  blocking collectives  172 us (23%)
  matrix products  149 us (20%)
  other arithmetic  56 us (7%)
  local copies, waits for them, and re-layouts  32.6 us (4%)
  between operations  16.9 us (2%)
    psum x1, waiting for transfers between devices, device_step(): lax.psum(jnp.einsum('tv,vd->td', d_logits, table_part, preferred_element_...  138 us
    psum x1, waiting for transfers between devices, device_step(): x_emb = lax.psum(emb_rows, 'model').astype(jnp.float32)  92.7 us
    unnamed x1, blocking collectives  69.2 us
    psum x1, blocking collectives, device_step(): tok_stats = lax.psum(part_stats, 'model')  56.2 us
    pmax x1, blocking collectives, device_step(): row_max = lax.pmax(jnp.max(logits, axis=-1), 'model')  33.9 us
    all_gather x1, waiting for transfers between devices, device_step(): table_part = lax.all_gather(table_shard, 'fsdp', axis=0, tiled=True)  31.4 us
    all_gather x1, waiting for transfers between devices, device_step(): w_gate = lax.all_gather(gate_shard, 'fsdp', axis=0, tiled=True)  26.3 us
    scatter-add x1, other arithmetic, device_step(): jax.ops.segment_sum(jnp.where(id_inside[:, None], d_x, 0.0), safe_ids, nu...  20.3 us
  transfers between devices with their start and end apart: 10, of which 6 were waited for; matrix products, arithmetic and copies ran while one was open for 26% of the time, Pallas kernels for 0%

commit v1 on v0

v1 whole, which is shorter than its diff:
```python
import functools

import jax
import jax.numpy as jnp
from jax import lax
from jax.experimental import pallas as pl
from jax.experimental.pallas import tpu as pltpu
from jax.sharding import PartitionSpec as P

EPS = 1e-6
F32 = jnp.float32
BF16 = jnp.bfloat16


def rms_scale(values, gain_vec):
    mean_sq = jnp.mean(values * values, axis=-1, keepdims=True)
    return values * lax.rsqrt(mean_sq + EPS) * gain_vec


def dot(spec, lhs, rhs):
    return jnp.einsum(spec, lhs, rhs, preferred_element_type=F32)


def add_rows_kernel(cap, count_ref, row_ref, add_ref, base_ref, out_ref):
    out_ref[...] = base_ref[...]

    def chunk(c, carry):
        def step(j, carry):
            row = row_ref[c * cap + j]
            out_ref[pl.ds(row, 1), :] += add_ref[pl.ds(c * cap + j, 1), :]
            return carry

        return lax.fori_loop(0, count_ref[c], step, carry)

    lax.fori_loop(0, count_ref.shape[0], chunk, 0)


def add_rows(base, rows, row_ids, counts, cap):
    vmem = pl.BlockSpec(memory_space=pltpu.VMEM)
    smem = pl.BlockSpec(memory_space=pltpu.SMEM)
    return pl.pallas_call(
        functools.partial(add_rows_kernel, cap),
        out_shape=jax.ShapeDtypeStruct(base.shape, base.dtype),
        in_specs=[smem, smem, vmem, vmem],
        out_specs=vmem,
        cost_estimate=pl.CostEstimate(flops=20_000_000, bytes_accessed=20_000_000, transcendentals=0),
    )(counts, row_ids, rows, base)


def solution(mesh):
    n_model, n_fsdp = mesh.shape["model"], mesh.shape["fsdp"]
    tok_spec = P("fsdp", None)
    row_spec = P(("model", "fsdp"), None)
    weight_spec = P("fsdp", None)

    def device_step(tok_ids, tok_labels, table_shard, gate_shard, up_shard, down_shard, gain_in, gain_out):
        me = lax.axis_index("model")
        group = tok_ids.shape[0] * tok_ids.shape[1]
        num_tokens = group * n_fsdp
        part = group // n_model
        rows, width = table_shard.shape
        pad_rows = -(-rows // 16) * 16
        block = rows * n_fsdp
        pad_block = pad_rows * n_fsdp
        hidden = gate_shard.shape[1]
        wg_rows, wd_rows = gate_shard.shape[0], down_shard.shape[0]
        sl = wd_rows // n_model
        fs = sl * n_fsdp

        table = lax.all_gather(jnp.pad(table_shard, ((0, pad_rows - rows), (0, 0))), "fsdp", axis=0, tiled=True)
        gate_all = gate_shard.reshape(wg_rows, n_fsdp, n_model, sl)
        up_all = up_shard.reshape(wg_rows, n_fsdp, n_model, sl)
        gate_sl = lax.dynamic_index_in_dim(gate_all, me, 2, keepdims=False).reshape(wg_rows, fs)
        up_sl = lax.dynamic_index_in_dim(up_all, me, 2, keepdims=False).reshape(wg_rows, fs)
        down_sl = lax.dynamic_slice_in_dim(down_shard, me * sl, sl, 0).reshape(wg_rows, fs)
        w_cat = jnp.concatenate([gate_sl, up_sl, down_sl], 0)
        w_cat = lax.all_gather(w_cat, ("model", "fsdp"), axis=0, tiled=True)
        w_cat = w_cat.reshape(n_model, n_fsdp, 3, wg_rows, fs)
        w_gate = w_cat[:, :, 0].reshape(n_model, width, fs)
        w_up = w_cat[:, :, 1].reshape(n_model, width, fs)
        w_down = w_cat[:, :, 2].reshape(n_model, fs, width)

        cap = part // 4
        ids = tok_ids.reshape(group)
        blk = (ids // block).reshape(n_model, part)
        loc = ids - me * block
        loc = (loc + (pad_rows - rows) * (loc // rows)).reshape(n_model, part)
        p_iota = jnp.arange(part, dtype=jnp.int32)
        m_iota = jnp.arange(n_model, dtype=jnp.int32)
        same = (blk[:, :, None] == blk[:, None, :]) & (p_iota[None, None, :] < p_iota[None, :, None])
        rank = jnp.sum(same.astype(jnp.int32), axis=2)
        cnt = jnp.sum((blk[:, :, None] == m_iota).astype(jnp.int32), axis=1)
        own_cnt = jnp.sum((blk == me).astype(jnp.int32), axis=1)
        rounds = (lax.pmax(jnp.max(cnt), "fsdp") + cap - 1) // cap
        j_iota = jnp.arange(cap, dtype=jnp.int32)
        my_blk = lax.dynamic_index_in_dim(blk, me, 0, keepdims=False)
        my_rank = lax.dynamic_index_in_dim(rank, me, 0, keepdims=False)

        def slots(k):
            hit = (blk[:, None, :] == me) & (rank[:, None, :] == (j_iota + k * cap)[None, :, None])
            return jnp.sum(jnp.where(hit, loc[:, None, :], 0), axis=2).reshape(n_model * cap)

        def pick(k):
            place = my_blk * cap + my_rank - k * cap
            place = jnp.where((my_rank >= k * cap) & (my_rank < (k + 1) * cap), place, -1)
            return place[:, None] == jnp.arange(n_model * cap, dtype=jnp.int32)[None, :]

        def fetch(k):
            got = lax.all_to_all(jnp.take(table, slots(k), axis=0), "model", 0, 0, tiled=True)
            return dot("ij,jd->id", pick(k).astype(BF16), got)

        def give(k, d_x, base):
            send = jnp.einsum("ij,id->jd", pick(k).astype(F32), d_x, precision=lax.Precision.HIGHEST, preferred_element_type=F32)
            got = lax.all_to_all(send, "model", 0, 0, tiled=True)
            return add_rows(base, got, slots(k), jnp.clip(own_cnt - k * cap, 0, cap), cap)

        x_emb = fetch(0)
        x_emb = lax.while_loop(lambda c: c[0] < rounds, lambda c: (c[0] + 1, c[1] + fetch(c[0])), (jnp.int32(1), x_emb))[1]

        normed_in, norm_in_back = jax.vjp(lambda values: rms_scale(values, gain_in), x_emb)
        a_bf = normed_in.astype(BF16)
        a_all = lax.all_gather(a_bf, "model", axis=0, tiled=True)
        gate_f = dot("td,mdf->tmf", a_bf, w_gate).astype(BF16).astype(F32)
        up_f = dot("td,mdf->tmf", a_bf, w_up).astype(BF16).astype(F32)
        gate_sig = jax.nn.sigmoid(gate_f)
        silu_gate = gate_f * gate_sig
        act_bf = (silu_gate * up_f).astype(BF16)
        mlp_out = dot("tmf,mfd->td", act_bf, w_down).astype(BF16)
        h_res = x_emb + mlp_out.astype(F32)
        hn_f, norm_out_back = jax.vjp(lambda values: rms_scale(values, gain_out), h_res)
        hn_bf = lax.all_gather(hn_f.astype(BF16), "model", axis=0, tiled=True)

        labels = tok_labels.reshape(group)
        lab = labels - me * block
        lab_in = (lab >= 0) & (lab < block)
        lab = jnp.where(lab_in, lab + (pad_rows - rows) * (lab // rows), -1)
        col = lax.broadcasted_iota(jnp.int32, (group, pad_block), 1)
        logits = dot("td,vd->tv", hn_bf, table)
        logits = jnp.where(col % pad_rows < rows, logits, -jnp.inf)
        loc_max = jnp.max(logits, axis=-1)
        loc_sum = jnp.sum(jnp.exp(logits - loc_max[:, None]), axis=-1)
        onehot = col == lab[:, None]
        loc_lab = jnp.sum(jnp.where(onehot, logits, 0.0), axis=-1)
        stats = lax.all_gather(jnp.stack([loc_max, loc_sum, loc_lab]), "model", axis=0)
        row_max = jnp.max(stats[:, 0], axis=0)
        sum_exp = jnp.sum(stats[:, 1] * jnp.exp(stats[:, 0] - row_max), axis=0)
        tok_loss = row_max + jnp.log(sum_exp) - jnp.sum(stats[:, 2], axis=0)
        loss_part = jnp.sum(tok_loss)
        soft = jnp.exp(logits - row_max[:, None]) / sum_exp[:, None]
        d_logits = (jnp.where(onehot, soft - 1.0, soft) / num_tokens).astype(BF16)
        d_hn = lax.psum_scatter(dot("tv,vd->td", d_logits, table), "model", scatter_dimension=0, tiled=True)
        d_head = dot("tv,td->vd", d_logits, hn_bf)

        d_hidden = norm_out_back(d_hn)[0]
        d_mlp = d_hidden.astype(BF16)
        dm_all = lax.all_gather(d_mlp, "model", axis=0, tiled=True)
        d_act = dot("td,mfd->tmf", d_mlp, w_down)
        silu_back = gate_sig * (1.0 + gate_f * (1.0 - gate_sig))
        d_gate = (d_act * up_f * silu_back).astype(BF16)
        d_up = (d_act * silu_gate).astype(BF16)
        d_normed = dot("tmf,mdf->td", d_gate, w_gate) + dot("tmf,mdf->td", d_up, w_up)
        d_x = d_hidden + norm_in_back(d_normed)[0]
        grad_block = give(0, d_x, d_head)
        grad_block = lax.while_loop(lambda c: c[0] < rounds, lambda c: (c[0] + 1, give(c[0], d_x, c[1])), (jnp.int32(1), grad_block))[1]
        grad_table = lax.psum_scatter(grad_block, "fsdp", scatter_dimension=0, tiled=True)[:rows]

        wg_s = lax.dynamic_index_in_dim(w_gate, me, 0, keepdims=False)
        wu_s = lax.dynamic_index_in_dim(w_up, me, 0, keepdims=False)
        wd_s = lax.dynamic_index_in_dim(w_down, me, 0, keepdims=False)
        gs = dot("td,df->tf", a_all, wg_s).astype(BF16).astype(F32)
        us = dot("td,df->tf", a_all, wu_s).astype(BF16).astype(F32)
        sig_s = jax.nn.sigmoid(gs)
        silu_s = gs * sig_s
        act_s = (silu_s * us).astype(BF16)
        d_act_s = dot("td,fd->tf", dm_all, wd_s)
        d_gate_s = (d_act_s * us * (sig_s * (1.0 + gs * (1.0 - sig_s)))).astype(BF16)
        d_up_s = (d_act_s * silu_s).astype(BF16)
        gg = dot("td,tf->df", a_all, d_gate_s).reshape(n_fsdp, wg_rows, fs)
        gu = dot("td,tf->df", a_all, d_up_s).reshape(n_fsdp, wg_rows, fs)
        gd = dot("tf,td->fd", act_s, dm_all).reshape(n_fsdp, wg_rows, fs)
        gl = jnp.full((n_fsdp, 8, fs), loss_part)
        cat = jnp.concatenate([gg, gu, gd, gl], 1).reshape(-1, fs)
        cat = lax.psum_scatter(cat, "fsdp", scatter_dimension=0, tiled=True)
        loss = cat[3 * wg_rows, 0] / num_tokens
        cat = lax.all_gather(cat, "model", axis=0)[:, : 3 * wg_rows].reshape(n_model, 3, wg_rows, fs)
        grad_gate = cat[:, 0].reshape(n_model, wg_rows, n_fsdp, sl).transpose(1, 2, 0, 3).reshape(wg_rows, hidden)
        grad_up = cat[:, 1].reshape(n_model, wg_rows, n_fsdp, sl).transpose(1, 2, 0, 3).reshape(wg_rows, hidden)
        grad_down = cat[:, 2].reshape(wd_rows, width)
        return loss, grad_table, grad_gate, grad_up, grad_down

    return jax.shard_map(device_step, mesh=mesh, in_specs=(tok_spec, tok_spec, row_spec, weight_spec, weight_spec, weight_spec, P(), P()), out_specs=(P(), row_spec, weight_spec, weight_spec, weight_spec), check_vma=False)
```

time: 755 us -> 599 us (0.79)
  blocking collectives: 172 us -> 26.2 us
  matrix products: 149 us -> 58.1 us
  waiting for transfers between devices: 320 us -> 395 us
  other arithmetic: 56 us -> 29.6 us
  local copies, waits for them, and re-layouts: 32.6 us -> 44.9 us
  Pallas kernels: 0 us -> 8.15 us
  starting transfers between devices: 5.05 us -> 12.6 us
    psum x2 -> x0, waiting for transfers between devices: 230 us -> none  [the longest x1 138 us: device_step(): lax.psum(jnp.einsum('tv,vd->td', d_logits, table_part, preferred_element_...]
    all_gather x4 -> x6, waiting for transfers between devices: 87 us -> 234 us  [the longest x1 45.1 us: device_step(): lax.all_gather(cat, 'model', axis=0)[:, :3 * wg_rows]]
    reduce_scatter x3 -> x2, waiting for transfers between devices: 0.01 us -> 121 us  [the longest x1 83.8 us: device_step(): lax.psum_scatter(dot('tv,vd->td', d_logits, table), 'model', scatter_dime...]
    dot_general x12 -> x17, matrix products: 149 us -> 58.1 us  [the longest x16 56.1 us: dot(): return jnp.einsum(spec, lhs, rhs, preferred_element_type=F32)]
    unnamed x1 -> x0, blocking collectives: 69.2 us -> none
    psum x2 -> x0, blocking collectives: 69.2 us -> none  [the longest x1 56.2 us: device_step(): tok_stats = lax.psum(part_stats, 'model')]
    pmax x1, blocking collectives: 33.9 us -> 8.12 us  [device_step(): rounds = (lax.pmax(jnp.max(cnt), 'fsdp') + cap - 1) // cap]
    unnamed x10, waiting for transfers between devices: 2.5 us -> 27.7 us
  transfers between devices with their start and end apart: 10 -> 11, of which waited for: 6 -> 11; matrix products, arithmetic and copies ran while one was open for 26% -> 10% of each run, Pallas kernels for 0% -> 1%
where the time goes in v1:
time: 599 us; the launch traced here: 591 us
  waiting for transfers between devices  395 us (66%)
  matrix products  58.1 us (10%)
  local copies, waits for them, and re-layouts  44.9 us (7%)
  other arithmetic  29.6 us (5%)
  blocking collectives  26.2 us (4%)
  between operations  16.4 us (3%)
  starting transfers between devices  12.6 us (2%)
  Pallas kernels  8.15 us (1%)
    reduce_scatter x1, waiting for transfers between devices, device_step(): lax.psum_scatter(dot('tv,vd->td', d_logits, table), 'model', scatter_dime...  83.8 us
    dot_general x16, matrix products, dot(): return jnp.einsum(spec, lhs, rhs, preferred_element_type=F32)  56.1 us
    all_gather x1, waiting for transfers between devices, device_step(): lax.all_gather(cat, 'model', axis=0)[:, :3 * wg_rows]  45.1 us
    all_gather x1, waiting for transfers between devices, device_step(): w_cat = lax.all_gather(w_cat, ('model', 'fsdp'), axis=0, tiled=True)  44.8 us
    all_gather x1, waiting for transfers between devices, device_step(): a_all = lax.all_gather(a_bf, 'model', axis=0, tiled=True)  44.4 us
    all_gather x1, waiting for transfers between devices, device_step(): hn_bf = lax.all_gather(hn_f.astype(BF16), 'model', axis=0, tiled=True)  41.2 us
    reduce_scatter x1, waiting for transfers between devices, device_step(): lax.psum_scatter(grad_block, 'fsdp', scatter_dimension=0, tiled=True)[:rows]  37.3 us
    all_gather x1, waiting for transfers between devices, device_step(): dm_all = lax.all_gather(d_mlp, 'model', axis=0, tiled=True)  32.9 us
  transfers between devices with their start and end apart: 11, of which 11 were waited for; matrix products, arithmetic and copies ran while one was open for 10% of the time, Pallas kernels for 1%

profile of v1, /device:TPU:1, one launch (start us, length us, event | category | flops | bytes accessed | tf_op | source)
XLA Modules:
  0.0 590.8 jit_solution(2884018771714846081)
XLA Ops:
  15.4 26.0 %all-gather.10.cloned.1.call-done = bf16[2048,768]{1,0:T(8,128)(2,1)} async-done(((bf16[256,768]{1,0:T(8,128)(2,1)}), bf16[2048,768]{1,0:T(8,128)(2,1)}) %all-gather.10.cloned.1.call-update) | async-done | bytes 3145744 | tf_op jit(solution)/shard_map/all_gather | solution.py:70
  41.3 5.4 gather_fusion.1
  49.0 6.7 %all-to-all-start.2 = ((bf16[16,32,768]{2,1,0:T(8,128)(2,1)}), bf16[16,32,768]{2,1,0:T(8,128)(2,1)}, u32[]{:S(2)}, u32[]{:S(2)}) async-start(bf16[16,32,768]{2,1,0:T(8,128)(2,1)} %broadcast_select_fusion.1), calls=%async_computation.2 | async-start | bytes 1572864 | tf_op jit(solution)/shard_map/all_to_all | solution.py:109
  56.8 8.1 %pmax.7 = s32[]{:T(128)} all-reduce(s32[]{:T(128)} %reduce_max.27), channel_id=1, replica_groups=mesh['model'=16,'fsdp'=8] {'fsdp'}, use_global_device_ids=true, to_apply=%region_4.5 | all-reduce | flops 1 | bytes 8 | tf_op jit(solution)/shard_map/pmax | solution.py:94
  74.0 44.8 %all-gather.14.cloned.1.call-done = bf16[36864,128]{1,0:T(8,128)(2,1)} async-done(((bf16[288,128]{1,0:T(8,128)(2,1)}), bf16[36864,128]{1,0:T(8,128)(2,1)}) %all-gather.14.cloned.1.call-update) | async-done | bytes 9437200 | tf_op jit(solution)/shard_map/all_gather | solution.py:77
  118.8 5.8 fusion.85
  127.8 6.4 %reshape_squeeze.20 = bf16[16,128,768]{2,1,0:T(8,128)(2,1)} reshape(bf16[16,8,1,96,128]{4,3,2,1,0:T(8,128)(2,1)} %get-tuple-element.249) | data formatting | bytes 6291456 | tf_op jit(solution)/shard_map/reshape;squeeze | solution.py:81
  141.8 41.2 %all-gather.16.cloned.1.call-done = bf16[2048,768]{1,0:T(8,128)(2,1)} async-done(((bf16[128,768]{1,0:T(8,128)(2,1)}), bf16[2048,768]{1,0:T(8,128)(2,1)}) %all-gather.16.cloned.1.call-update) | async-done | bytes 3145744 | tf_op jit(solution)/shard_map/all_gather | solution.py:131
  183.0 9.1 %fusion.87 = (f32[2048]{0:T(1024)S(1)}, f32[2048,2048]{0,1:T(8,128)S(1)}) fusion(bf16[2048,768]{1,0:T(8,128)(2,1)} %all-gather.16.cloned.1.call-done, bf16[2048,768]{1,0:T(8,128)(2,1)S(1)} %get-tuple-element.484, s32[2048]{0:T(1024)} %get-tuple-element.267, s32[2048]{0:T(1024)} %get-tuple-element.268, pred[2048]{0:T(1024)(128)(4,1)} %fusion.68), kind=kOutput, calls=%fused_computation.178 | convolution fusion | flops 6459226112 | bytes 23095296 | tf_op jit(solution)/shard_map/td,vd->tv/dot_general | solution.py:21
  192.1 4.6 exponential_reduce_fusion
  196.8 18.1 %all-gather.2 = f32[16,3,2048]{2,1,0:T(4,128)S(1)} all-gather(f32[1,3,2048]{2,1,0:T(4,128)S(1)} %maximum_bitcast_fusion), channel_id=2, replica_groups=mesh['model'=16,'fsdp'=8] {'model'}, dimensions={0}, use_global_device_ids=true | all-gather | bytes 417792 | tf_op jit(solution)/shard_map/all_gather | solution.py:144
  215.9 5.3 fusion.8
  224.5 8.9 %fusion.89 = f32[2048,768]{1,0:T(8,128)} fusion(bf16[2048,2048]{0,1:T(8,128)(2,1)S(1)} %fusion.8, bf16[2048,768]{1,0:T(8,128)(2,1)S(1)} %get-tuple-element.484), kind=kOutput, calls=%fused_computation.180 | convolution fusion | flops 6442450944 | bytes 17825792 | tf_op jit(solution)/shard_map/tv,vd->td/dot_general | solution.py:21
  234.2 83.8 %reduce-scatter.3.cloned.1.call-done = f32[128,768]{1,0:T(8,128)} async-done(((f32[2048,768]{1,0:T(8,128)}), f32[128,768]{1,0:T(8,128)}) %reduce-scatter.3.cloned.1.call-update) | async-done | bytes 393232 | tf_op jit(solution)/shard_map/reduce_scatter | solution.py:151
  323.7 44.4 %all-gather.12.cloned.1.call-done = bf16[2048,768]{1,0:T(8,128)(2,1)} async-done(((bf16[128,768]{1,0:T(8,128)(2,1)}), bf16[2048,768]{1,0:T(8,128)(2,1)}) %all-gather.12.cloned.1.call-update) | async-done | bytes 3145744 | tf_op jit(solution)/shard_map/all_gather | solution.py:122
  368.1 4.0 fusion.10
  383.7 32.9 %all-gather.18.cloned.1.call-done = bf16[2048,768]{1,0:T(8,128)(2,1)} async-done(((bf16[128,768]{1,0:T(8,128)(2,1)}), bf16[2048,768]{1,0:T(8,128)(2,1)}) %all-gather.18.cloned.1.call-update) | async-done | bytes 3145744 | tf_op jit(solution)/shard_map/all_gather | solution.py:156
  428.1 4.8 all-to-all-start.3
  433.2 11.7 %fusion.90.base_ref = f32[2048,768]{1,0:T(8,128)} fusion(bf16[2048,2048]{0,1:T(8,128)(2,1)} %copy-done.12, bf16[2048,768]{1,0:T(8,128)(2,1)} %all-gather.16.cloned.1.call-done), kind=kOutput, calls=%fused_computation.181 | convolution fusion | flops 6442450944 | bytes 17825792 | tf_op jit(solution)/shard_map/tv,td->vd/dot_general | solution.py:21
  444.9 8.9 %all-to-all-done.3 = f32[16,32,768]{2,1,0:T(8,128)S(1)} async-done(((f32[16,32,768]{2,1,0:T(8,128)}), f32[16,32,768]{2,1,0:T(8,128)S(1)}, u32[]{:S(2)}, u32[]{:S(2)}) %all-to-all-start.3) | async-done | bytes 1572896 | tf_op jit(solution)/shard_map/all_to_all | solution.py:114
  455.0 8.1 %shard_map.119 = f32[2048,768]{1,0:T(8,128)} custom-call(s32[16]{0:T(128)} %broadcast_clamp_fusion.count_ref, s32[512]{0:T(512)} %reshape.397.row_ref, f32[512,768]{1,0:T(8,128)} %bitcast.161, f32[2048,768]{1,0:T(8,128)} %fusion.90.base_ref), custom_call_target="tpu_custom_call" | custom-call | flops 20000000 | bytes 20000000 | tf_op jit(solution)/shard_map/pallas_call | solution.py:41
  463.1 26.4 %all-reduce.4.cloned.1.call-done = f32[2368,128]{1,0:T(8,128)} async-done(((f32[2368,128]{1,0:T(8,128)}), f32[2368,128]{1,0:T(8,128)}) %all-reduce.4.cloned.1.call-update) | async-done | bytes 1212432
  493.1 45.1 %all-gather.20.cloned.1.call-done = f32[4736,128]{1,0:T(8,128)} async-done(((f32[296,128]{1,0:T(8,128)}), f32[4736,128]{1,0:T(8,128)}) %all-gather.20.cloned.1.call-update) | async-done | bytes 2424848 | tf_op jit(solution)/shard_map/all_gather | solution.py:185
  546.5 37.3 %reduce-scatter.5.cloned.1.call-done = f32[256,768]{1,0:T(8,128)} async-done(((f32[2048,768]{1,0:T(8,128)}), f32[256,768]{1,0:T(8,128)}) %reduce-scatter.5.cloned.1.call-update) | async-done | bytes 786448 | tf_op jit(solution)/shard_map/reduce_scatter | solution.py:165
  (207 shorter events, 76.5 us)
Async XLA Ops:
  7.2 34.1 %all-gather.10.cloned.1.call-start = ((), (), s32[]{:S(2)}) async-start(), calls=%async_computation.6 | async-start | bytes 3538944 | tf_op jit(solution)/shard_map/all_gather | solution.py:70
  9.1 109.7 %all-gather.14.cloned.1.call-start = ((), (), s32[]{:S(2)}) async-start(), calls=%async_computation.8 | async-start | bytes 9510912 | tf_op jit(solution)/shard_map/all_gather | solution.py:77
  49.0 20.7 %all-to-all-start.2 = ((bf16[16,32,768]{2,1,0:T(8,128)(2,1)}), bf16[16,32,768]{2,1,0:T(8,128)(2,1)}, u32[]{:S(2)}, u32[]{:S(2)}) async-start(bf16[16,32,768]{2,1,0:T(8,128)(2,1)} %broadcast_select_fusion.1), calls=%async_computation.2 | async-start | bytes 1572864 | tf_op jit(solution)/shard_map/all_to_all | solution.py:109
  55.8 127.3 %all-gather.16.cloned.1.call-start = ((), (), s32[]{:S(2)}) async-start(), calls=%async_computation.9 | async-start | bytes 3342336 | tf_op jit(solution)/shard_map/all_gather | solution.py:131
  139.1 178.8 %reduce-scatter.3.cloned.1.call-start = ((), (), s32[]{:S(2)}) async-start(), calls=%async_computation.10 | async-start | bytes 6684672 | tf_op jit(solution)/shard_map/reduce_scatter | solution.py:151
  233.5 84.5 %copy-start.15 = (f32[128,768]{1,0:T(8,128)S(1)}, f32[128,768]{1,0:T(8,128)}, u32[]{:S(2)}) copy-start(f32[128,768]{1,0:T(8,128)} %copy-done.14) | copy-start | bytes 1179652
  233.5 84.5 %copy-start.35 = (f32[768]{0:T(1024)S(1)}, f32[768]{0:T(1024)}, u32[]{:S(2)}) copy-start(f32[768]{0:T(1024)} %param.19) | copy-start | bytes 9220
  233.5 85.6 %copy-start.58 = (f32[128]{0:T(128)S(1)}, f32[128]{0:T(128)}, u32[]{:S(2)}) copy-start(f32[128]{0:T(128)} %copy-done.57) | copy-start | bytes 1540
  233.5 85.6 %copy-start.45 = (f32[128]{0:T(128)S(1)}, f32[128]{0:T(128)}, u32[]{:S(2)}) copy-start(f32[128]{0:T(128)} %copy-done.44) | copy-start | bytes 1540
  233.5 87.7 %copy-start.30 = (s32[16,32]{1,0:T(8,128)S(1)}, s32[16,32]{1,0:T(8,128)}, u32[]{:S(2)}) copy-start(s32[16,32]{1,0:T(8,128)} %copy-done.29) | copy-start | bytes 6148
  233.5 88.4 %copy-start.56 = (u32[128]{0:T(128)S(1)}, u32[128]{0:T(128)}, u32[]{:S(2)}) copy-start(u32[128]{0:T(128)} %constant.176) | copy-start | bytes 1540
  233.5 89.6 %copy-start.54 = (s32[16]{0:T(128)S(1)}, s32[16]{0:T(128)}, u32[]{:S(2)}) copy-start(s32[16]{0:T(128)} %get-tuple-element.438) | copy-start | bytes 196
  233.5 134.5 %all-gather.12.cloned.1.call-start = ((), (), s32[]{:S(2)}) async-start(), calls=%async_computation.7 | async-start | bytes 3342336 | tf_op jit(solution)/shard_map/all_gather | solution.py:122
  234.1 182.5 %all-gather.18.cloned.1.call-start = ((), (), s32[]{:S(2)}) async-start(), calls=%async_computation.11 | async-start | bytes 3342336 | tf_op jit(solution)/shard_map/all_gather | solution.py:156
  320.9 168.6 %all-reduce.4.cloned.1.call-start = ((), (), s32[]{:S(2)}) async-start(), calls=%async_computation.14 | async-start | bytes 2424832
  428.1 25.7 %all-to-all-start.3 = ((f32[16,32,768]{2,1,0:T(8,128)}), f32[16,32,768]{2,1,0:T(8,128)S(1)}, u32[]{:S(2)}, u32[]{:S(2)}) async-start(f32[16,32,768]{2,1,0:T(8,128)} %bitcast.34), calls=%async_computation.4 | async-start | bytes 3145728 | tf_op jit(solution)/shard_map/all_to_all | solution.py:114
  432.9 105.2 %all-gather.20.cloned.1.call-start = ((), (), s32[]{:S(2)}) async-start(), calls=%async_computation.13 | async-start | bytes 2576384 | tf_op jit(solution)/shard_map/all_gather | solution.py:185
  455.0 36.2 %copy-start.6 = (f32[128,768]{1,0:T(8,128)S(1)}, f32[128,768]{1,0:T(8,128)}, u32[]{:S(2)}) copy-start(f32[128,768]{1,0:T(8,128)} %copy-done.5) | copy-start | bytes 1179652
  455.0 36.2 %copy-start.24 = (s32[2048]{0:T(1024)S(1)}, s32[2048]{0:T(1024)}, u32[]{:S(2)}) copy-start(s32[2048]{0:T(1024)} %get-tuple-element.510) | copy-start | bytes 24580
  455.0 36.2 %copy-start.37 = (s32[128]{0:T(128)S(1)}, s32[128]{0:T(128)}, u32[]{:S(2)}) copy-start(s32[128]{0:T(128)} %get-tuple-element.517) | copy-start | bytes 1540
  455.0 36.2 %copy-start.38 = (s32[128]{0:T(128)S(1)}, s32[128]{0:T(128)}, u32[]{:S(2)}) copy-start(s32[128]{0:T(128)} %get-tuple-element.518) | copy-start | bytes 1540
  455.0 36.2 %copy-start.55 = (s32[16]{0:T(128)S(1)}, s32[16]{0:T(128)}, u32[]{:S(2)}) copy-start(s32[16]{0:T(128)} %get-tuple-element.438) | copy-start | bytes 196
  491.1 92.7 %reduce-scatter.5.cloned.1.call-start = ((), (), s32[]{:S(2)}) async-start(), calls=%async_computation.12 | async-start | bytes 7077888 | tf_op jit(solution)/shard_map/reduce_scatter | solution.py:165
  542.7 41.1 %copy-start.1 = (bf16[256,768]{1,0:T(8,128)(2,1)S(1)}, bf16[256,768]{1,0:T(8,128)(2,1)}, u32[]{:S(2)}) copy-start(bf16[256,768]{1,0:T(8,128)(2,1)} %param.17) | copy-start | bytes 1179652
  (43 other events, 168.4 us)
Sparse Core Ops, SparseCore 0:
  10.3 31.0 all-gather.9
  44.9 73.7 all-gather.13
  139.2 43.7 all-gather.15
  233.7 84.2 reduce-scatter.2
  320.5 47.5 all-gather.11
  370.1 46.4 all-gather.17
  428.2 61.2 all-reduce.3
  492.2 45.8 all-gather.19
  541.1 42.6 reduce-scatter.4
